TPU v7x, 32 devices: a whole 2x2x4 slice. The times are simulated.
32 devices in a mesh: seq: 4 (over x, core), fsdp: 8 (over z, y).
Axes of the slice: x: 2, y: 2, z: 4, core: 2. Of those that a mesh axis runs over, the one named last changes fastest.
Arguments:
- tokens: bfloat16 [8, 1024, 2048], P('fsdp', 'seq'), may hold values from -6 to 6
- targets: bfloat16 [8, 1024, 2048], P('fsdp', 'seq'), may hold values from -6 to 6
- lengths: int32 [8], replicated, may hold values from 1 to 1024, 6144 in all
- w_qkv: float32 [2048, 3, 2048], P('fsdp', None, 'seq'), may hold values from -0.125 to 0.125
- w_out: float32 [2048, 2048], P('seq', 'fsdp'), may hold values from -1 to 1
- w_gateup: float32 [2048, 2, 8192], P('fsdp', None, 'seq'), may hold values from -0.125 to 0.125
- w_down: float32 [8192, 2048], P('seq', 'fsdp'), may hold values from -0.0625 to 0.0625
- mom_qkv: float32 [2048, 3, 2048], P('fsdp', None, 'seq'), may hold values from -0.0390625 to 0.0390625
- mom_out: float32 [2048, 2048], P('seq', 'fsdp'), may hold values from -0.0234375 to 0.0234375
- mom_gateup: float32 [2048, 2, 8192], P('fsdp', None, 'seq'), may hold values from -0.0390625 to 0.0390625
- mom_down: float32 [8192, 2048], P('seq', 'fsdp'), may hold values from -0.078125 to 0.078125
- avg_qkv: float32 [2048, 3, 2048], P('fsdp', None, 'seq'), may hold values from -0.125 to 0.125
- avg_out: float32 [2048, 2048], P('seq', 'fsdp'), may hold values from -1 to 1
- avg_gateup: float32 [2048, 2, 8192], P('fsdp', None, 'seq'), may hold values from -0.125 to 0.125
- avg_down: float32 [8192, 2048], P('seq', 'fsdp'), may hold values from -0.0625 to 0.0625
Outputs:
- output: bfloat16 [8, 1024, 2048], P('fsdp', 'seq')
- input_grad: bfloat16 [8, 1024, 2048], P('fsdp', 'seq')
- loss: float32 [], replicated
- new_qkv: float32 [2048, 3, 2048], P('fsdp', None, 'seq')
- new_out: float32 [2048, 2048], P('seq', 'fsdp')
- new_gateup: float32 [2048, 2, 8192], P('fsdp', None, 'seq')
- new_down: float32 [8192, 2048], P('seq', 'fsdp')
- newmom_qkv: float32 [2048, 3, 2048], P('fsdp', None, 'seq')
- newmom_out: float32 [2048, 2048], P('seq', 'fsdp')
- newmom_gateup: float32 [2048, 2, 8192], P('fsdp', None, 'seq')
- newmom_down: float32 [8192, 2048], P('seq', 'fsdp')
- newavg_qkv: float32 [2048, 3, 2048], P('fsdp', None, 'seq')
- newavg_out: float32 [2048, 2048], P('seq', 'fsdp')
- newavg_gateup: float32 [2048, 2, 8192], P('fsdp', None, 'seq')
- newavg_down: float32 [8192, 2048], P('seq', 'fsdp')
Inputs may be any that keep to these rules, and one draw needn't show every extreme that they name: lengths[s] valid tokens stand first in sequence s's 1024 slots, padding after; they sum to 6144 and one equals 1024.
All inputs are finite; a program needn't handle non-finite values.
Results may differ from a plain program's by a relative error of at most 0.015.
Values may be sent and summed in bfloat16 or wider, within the bound.
A program may use at most 256 MiB of HBM per device.

v0:
```python
import jax
import jax.numpy as jnp
from jax import lax
from jax.sharding import PartitionSpec as P

HD = 128
EPS = 1e-05
ROPE_BASE = 10000.0
MOMENT = 0.9
KEEP = 0.95
NEG = -1e30


def layer_norm(values):
    centred = values - jnp.mean(values, axis=-1, keepdims=True)
    factor = lax.rsqrt(jnp.mean(centred * centred, axis=-1, keepdims=True) + EPS)
    return (centred * factor, factor)


def norm_back(grad, normed, factor):
    inner = jnp.mean(grad * normed, axis=-1, keepdims=True)
    return factor * (grad - jnp.mean(grad, axis=-1, keepdims=True) - normed * inner)


def rotary(span, width):
    half = width // 2
    freq = ROPE_BASE ** (-2.0 * jnp.arange(half, dtype=jnp.float32) / width)
    angle = jnp.arange(span, dtype=jnp.float32)[:, None] * freq[None, :]
    cosine = jnp.concatenate([jnp.cos(angle), jnp.cos(angle)], axis=-1)[:, None, :]
    sine = jnp.concatenate([jnp.sin(angle), jnp.sin(angle)], axis=-1)[:, None, :]
    return (cosine, sine)


def rotate(values):
    half = values.shape[-1] // 2
    return jnp.concatenate([-values[..., half:], values[..., :half]], axis=-1)


def unrotate(values):
    half = values.shape[-1] // 2
    return jnp.concatenate([values[..., half:], -values[..., :half]], axis=-1)


def allowed_mask(first_row, block_rows, span, length):
    positions = jnp.arange(span, dtype=jnp.int32)
    query_pos = first_row + jnp.arange(block_rows, dtype=jnp.int32)
    return (positions[None, :] <= query_pos[:, None]) & (positions[None, :] < length)


def attend_forward(queries, keys_rot, values_v, length):
    span = queries.shape[0]
    block_rows = min(512, span)
    scale = queries.shape[2] ** (-0.5)

    def one_block(first_row):
        rows_q = lax.dynamic_slice_in_dim(queries, first_row, block_rows, 0)
        scores = (
            jnp.einsum("qhd,khd->hqk", rows_q, keys_rot, preferred_element_type=jnp.float32) * scale
        )
        scores = jnp.where(allowed_mask(first_row, block_rows, span, length)[None], scores, NEG)
        highest = jnp.max(scores, axis=-1, keepdims=True)
        expvals = jnp.exp(scores - highest)
        totals = jnp.sum(expvals, axis=-1, keepdims=True)
        attn_probs = (expvals / totals).astype(jnp.bfloat16)
        outs = jnp.einsum("hqk,khd->qhd", attn_probs, values_v, preferred_element_type=jnp.float32)
        return (outs, highest[..., 0] + jnp.log(totals[..., 0]))

    starts = jnp.arange(span // block_rows) * block_rows
    outs, log_totals = lax.map(one_block, starts)
    return (outs.reshape(span, queries.shape[1], queries.shape[2]), log_totals)


def attend_back(queries, keys_rot, values_v, grad_out, log_totals, length):
    span = queries.shape[0]
    block_rows = min(512, span)
    scale = queries.shape[2] ** (-0.5)
    starts = jnp.arange(span // block_rows) * block_rows

    def one_block(carry, item):
        first_row, lse_block = item
        rows_q = lax.dynamic_slice_in_dim(queries, first_row, block_rows, 0)
        rows_g = lax.dynamic_slice_in_dim(grad_out, first_row, block_rows, 0)
        scores = (
            jnp.einsum("qhd,khd->hqk", rows_q, keys_rot, preferred_element_type=jnp.float32) * scale
        )
        allowed = allowed_mask(first_row, block_rows, span, length)[None]
        attn_probs = jnp.where(allowed, jnp.exp(scores - lse_block[..., None]), 0.0)
        probs_low = attn_probs.astype(jnp.bfloat16)
        grad_values = carry[1] + jnp.einsum(
            "hqk,qhd->khd", probs_low, rows_g, preferred_element_type=jnp.float32
        )
        grad_probs = jnp.einsum(
            "qhd,khd->hqk", rows_g, values_v, preferred_element_type=jnp.float32
        )
        inner = jnp.sum(attn_probs * grad_probs, axis=-1, keepdims=True)
        grad_scores = (attn_probs * (grad_probs - inner)).astype(jnp.bfloat16)
        grad_rows = (
            jnp.einsum("hqk,khd->qhd", grad_scores, keys_rot, preferred_element_type=jnp.float32)
            * scale
        )
        grad_keys = (
            carry[0]
            + jnp.einsum("hqk,qhd->khd", grad_scores, rows_q, preferred_element_type=jnp.float32)
            * scale
        )
        return ((grad_keys, grad_values), grad_rows)

    zeros_kv = jnp.zeros(keys_rot.shape, jnp.float32)
    (grad_keys, grad_values), grad_rows = lax.scan(
        one_block, (zeros_kv, zeros_kv), (starts, log_totals)
    )
    return (grad_rows.reshape(queries.shape), grad_keys, grad_values)


def advance(weight, moment, average, grad, rate):
    moment_new = MOMENT * moment + grad
    weight_new = weight - rate * (grad + MOMENT * moment_new)
    average_new = KEEP * average + (1.0 - KEEP) * weight_new
    return (weight_new, moment_new, average_new)


def on_device(
    tokens,
    targets,
    lengths,
    w_qkv,
    w_out,
    w_gateup,
    w_down,
    mom_qkv,
    mom_out,
    mom_gateup,
    mom_down,
    avg_qkv,
    avg_out,
    avg_gateup,
    avg_down,
):
    n_shards = lax.axis_size("seq")
    shard_index = lax.axis_index("seq")
    member = lax.axis_index("fsdp")
    own_rows = tokens.shape[1]
    span = own_rows * n_shards
    head_size = HD
    heads_here = w_qkv.shape[2] // head_size
    inputs = tokens[0].astype(jnp.float32)
    target = targets[0].astype(jnp.float32)
    own_length = lax.dynamic_index_in_dim(lengths, member, 0, keepdims=False)
    count = jnp.sum(lengths).astype(jnp.float32)
    own_pos = shard_index * own_rows + jnp.arange(own_rows, dtype=jnp.int32)
    valid = (own_pos < own_length).astype(jnp.float32)[:, None]
    low_weights = (
        w_qkv.astype(jnp.bfloat16),
        w_out.astype(jnp.bfloat16),
        w_gateup.astype(jnp.bfloat16),
        w_down.astype(jnp.bfloat16),
    )
    full_qkv, full_out, full_gateup, full_down = (
        lax.all_gather(low_weights[0], "fsdp", axis=0, tiled=True),
        lax.all_gather(low_weights[1], "fsdp", axis=1, tiled=True),
        lax.all_gather(low_weights[2], "fsdp", axis=0, tiled=True),
        lax.all_gather(low_weights[3], "fsdp", axis=1, tiled=True),
    )
    normed_one, factor_one = layer_norm(inputs)
    group_one = lax.all_gather(normed_one.astype(jnp.bfloat16), "seq", axis=0, tiled=True)
    qkv_all = jnp.einsum("td,djc->tjc", group_one, full_qkv, preferred_element_type=jnp.float32)
    cosine, sine = rotary(span, head_size)
    queries = qkv_all[:, 0].reshape(span, heads_here, head_size)
    keys_pre = qkv_all[:, 1].reshape(span, heads_here, head_size)
    queries = (queries * cosine + rotate(queries) * sine).astype(jnp.bfloat16)
    keys_rot = (keys_pre * cosine + rotate(keys_pre) * sine).astype(jnp.bfloat16)
    values_v = qkv_all[:, 2].reshape(span, heads_here, head_size).astype(jnp.bfloat16)
    attended, log_totals = attend_forward(queries, keys_rot, values_v, own_length)
    attended = attended.reshape(span, heads_here * head_size).astype(jnp.bfloat16)
    attn_term = jnp.dot(attended, full_out, preferred_element_type=jnp.float32)
    middle = inputs + lax.psum_scatter(
        attn_term.astype(jnp.bfloat16), "seq", scatter_dimension=0, tiled=True
    ).astype(jnp.float32)
    normed_two, factor_two = layer_norm(middle)
    group_two = lax.all_gather(normed_two.astype(jnp.bfloat16), "seq", axis=0, tiled=True)
    gate_up = jnp.einsum("td,djf->tjf", group_two, full_gateup, preferred_element_type=jnp.float32)
    gate = gate_up[:, 0]
    up_part = gate_up[:, 1]
    hidden = (jax.nn.silu(gate) * up_part).astype(jnp.bfloat16)
    ffn_term = jnp.dot(hidden, full_down, preferred_element_type=jnp.float32)
    result = middle + lax.psum_scatter(
        ffn_term.astype(jnp.bfloat16), "seq", scatter_dimension=0, tiled=True
    ).astype(jnp.float32)
    diff = (result - target) * valid
    loss = lax.psum(jnp.sum(diff * diff), ("seq", "fsdp")) / (2.0 * count)
    grad_result = diff / count
    full_qkv, full_out, full_gateup, full_down = (
        lax.all_gather(low_weights[0], "fsdp", axis=0, tiled=True),
        lax.all_gather(low_weights[1], "fsdp", axis=1, tiled=True),
        lax.all_gather(low_weights[2], "fsdp", axis=0, tiled=True),
        lax.all_gather(low_weights[3], "fsdp", axis=1, tiled=True),
    )
    contract_rows = (((0,), (0,)), ((), ()))
    contract_cols = (((1,), (1,)), ((), ()))
    group_dy = lax.all_gather(grad_result.astype(jnp.bfloat16), "seq", axis=0, tiled=True)
    grad_hidden = lax.dot_general(
        group_dy, full_down, contract_cols, preferred_element_type=jnp.float32
    )
    grad_down = lax.dot_general(hidden, group_dy, contract_rows, preferred_element_type=jnp.float32)
    sigma = jax.nn.sigmoid(gate)
    grad_gate = grad_hidden * up_part * sigma * (1.0 + gate * (1.0 - sigma))
    grad_up = grad_hidden * gate * sigma
    grad_gu = jnp.stack([grad_gate, grad_up], axis=1).astype(jnp.bfloat16)
    normed_grad_two = jnp.einsum(
        "tjf,djf->td", grad_gu, full_gateup, preferred_element_type=jnp.float32
    )
    grad_gateup = jnp.einsum("td,tjf->djf", group_two, grad_gu, preferred_element_type=jnp.float32)
    own_grad_two = lax.psum_scatter(
        normed_grad_two.astype(jnp.bfloat16), "seq", scatter_dimension=0, tiled=True
    ).astype(jnp.float32)
    grad_middle = grad_result + norm_back(own_grad_two, normed_two, factor_two)
    group_da = lax.all_gather(grad_middle.astype(jnp.bfloat16), "seq", axis=0, tiled=True)
    grad_att = lax.dot_general(
        group_da, full_out, contract_cols, preferred_element_type=jnp.float32
    )
    grad_att = grad_att.astype(jnp.bfloat16).reshape(span, heads_here, head_size)
    grad_out = lax.dot_general(
        attended, group_da, contract_rows, preferred_element_type=jnp.float32
    )
    grad_rows, grad_keys, grad_values = attend_back(
        queries, keys_rot, values_v, grad_att, log_totals, own_length
    )
    grad_rows = grad_rows * cosine + unrotate(grad_rows * sine)
    grad_keys = grad_keys * cosine + unrotate(grad_keys * sine)
    grad_qkv_all = jnp.stack(
        [grad_rows.reshape(span, -1), grad_keys.reshape(span, -1), grad_values.reshape(span, -1)],
        axis=1,
    ).astype(jnp.bfloat16)
    normed_grad_one = jnp.einsum(
        "tjc,djc->td", grad_qkv_all, full_qkv, preferred_element_type=jnp.float32
    )
    grad_qkv = jnp.einsum(
        "td,tjc->djc", group_one, grad_qkv_all, preferred_element_type=jnp.float32
    )
    own_grad_one = lax.psum_scatter(
        normed_grad_one.astype(jnp.bfloat16), "seq", scatter_dimension=0, tiled=True
    ).astype(jnp.float32)
    grad_inputs = grad_middle + norm_back(own_grad_one, normed_one, factor_one)
    summed_qkv, summed_out, summed_gateup, summed_down = (
        lax.psum_scatter(
            grad_qkv.astype(jnp.bfloat16), "fsdp", scatter_dimension=0, tiled=True
        ).astype(jnp.float32),
        lax.psum_scatter(
            grad_out.astype(jnp.bfloat16), "fsdp", scatter_dimension=1, tiled=True
        ).astype(jnp.float32),
        lax.psum_scatter(
            grad_gateup.astype(jnp.bfloat16), "fsdp", scatter_dimension=0, tiled=True
        ).astype(jnp.float32),
        lax.psum_scatter(
            grad_down.astype(jnp.bfloat16), "fsdp", scatter_dimension=1, tiled=True
        ).astype(jnp.float32),
    )
    new_qkv, newmom_qkv, newavg_qkv = advance(w_qkv, mom_qkv, avg_qkv, summed_qkv, 2.0)
    new_out, newmom_out, newavg_out = advance(w_out, mom_out, avg_out, summed_out, 20.0)
    new_gateup, newmom_gateup, newavg_gateup = advance(
        w_gateup, mom_gateup, avg_gateup, summed_gateup, 2.0
    )
    new_down, newmom_down, newavg_down = advance(w_down, mom_down, avg_down, summed_down, 1.0)
    return (
        result.astype(jnp.bfloat16)[None],
        grad_inputs.astype(jnp.bfloat16)[None],
        loss,
        new_qkv,
        new_out,
        new_gateup,
        new_down,
        newmom_qkv,
        newmom_out,
        newmom_gateup,
        newmom_down,
        newavg_qkv,
        newavg_out,
        newavg_gateup,
        newavg_down,
    )


def solution(mesh):
    placed = (
        P("fsdp", "seq", None),
        P("fsdp", "seq", None),
        P(),
        P("fsdp", None, "seq"),
        P("seq", "fsdp"),
        P("fsdp", None, "seq"),
        P("seq", "fsdp"),
        P("fsdp", None, "seq"),
        P("seq", "fsdp"),
        P("fsdp", None, "seq"),
        P("seq", "fsdp"),
        P("fsdp", None, "seq"),
        P("seq", "fsdp"),
        P("fsdp", None, "seq"),
        P("seq", "fsdp"),
    )
    return jax.shard_map(
        on_device,
        mesh=mesh,
        in_specs=placed,
        out_specs=(
            P("fsdp", "seq", None),
            P("fsdp", "seq", None),
            P(),
            P("fsdp", None, "seq"),
            P("seq", "fsdp"),
            P("fsdp", None, "seq"),
            P("seq", "fsdp"),
            P("fsdp", None, "seq"),
            P("seq", "fsdp"),
            P("fsdp", None, "seq"),
            P("seq", "fsdp"),
            P("fsdp", None, "seq"),
            P("seq", "fsdp"),
            P("fsdp", None, "seq"),
            P("seq", "fsdp"),
        ),
        check_vma=False,
    )
```

profile of v0, /device:TPU:0, one launch (start us, length us, event | category | flops | bytes accessed | tf_op | source)
XLA Modules:
  0.0 1588.2 jit_solution(3938071013215438621)
XLA Ops:
  19.5 30.2 %all-gather.9.cloned.1.call-done = bf16[1024,2048]{1,0:T(8,128)(2,1)} async-done(((bf16[256,2048]{1,0:T(8,128)(2,1)}), bf16[1024,2048]{1,0:T(8,128)(2,1)}) %all-gather.9.cloned.1.call-update) | async-done | bytes 4194320 | tf_op jit(solution)/shard_map/all_gather | solution.py:165
  49.7 102.1 %all-gather.11.cloned.1.call-done = bf16[2048,3,512]{0,2,1:T(8,128)(2,1)} async-done(((bf16[256,3,512]{0,2,1:T(8,128)(2,1)}), bf16[2048,3,512]{0,2,1:T(8,128)(2,1)}) %all-gather.11.cloned.1.call-update) | async-done | bytes 6291472 | tf_op jit(solution)/shard_map/all_gather | solution.py:159
  180.4 24.5 %while.29 = (s32[]{:T(128)}, bf16[2,512,4,128]{3,1,2,0:T(8,128)(2,1)}, f32[2,4,512]{2,1,0:T(4,128)S(1)}, s32[2]{0:T(128)S(1)}, s32[]{:T(128)}, /*index=5*/bf16[1...) while((s32[]{:T(128)}, ...), condition=%wide.region_5.6_spmd.clone, body=%wide.region_2.5_spmd.sunk.clone | while | flops 1099955712 | bytes 35199660 | solution.py:69
  215.1 42.9 %reduce-scatter.9.cloned.1.call-done = bf16[256,2048]{1,0:T(8,128)(2,1)} async-done(((bf16[1024,2048]{1,0:T(8,128)(2,1)}), bf16[256,2048]{1,0:T(8,128)(2,1)}) %reduce-scatter.9.cloned.1.call-update) | async-done | bytes 1048592 | tf_op jit(solution)/shard_map/reduce_scatter | solution.py:176
  270.4 25.8 %all-gather.15.cloned.1.call-done = bf16[1024,2048]{1,0:T(8,128)(2,1)} async-done(((bf16[256,2048]{1,0:T(8,128)(2,1)}), bf16[1024,2048]{1,0:T(8,128)(2,1)}) %all-gather.15.cloned.1.call-update) | async-done | bytes 4194320 | tf_op jit(solution)/shard_map/all_gather | solution.py:180
  296.2 229.9 %all-gather.17.cloned.1.call-done = bf16[2048,2,2048]{2,0,1:T(8,128)(2,1)} async-done(((bf16[256,2,2048]{2,0,1:T(8,128)(2,1)}), bf16[2048,2,2048]{2,0,1:T(8,128)(2,1)}) %all-gather.17.cloned.1.call-update) | async-done | bytes 16777232 | tf_op jit(solution)/shard_map/all_gather | solution.py:161
  526.1 21.5 %fusion.39 = f32[1024,2,2048]{2,0,1:T(8,128)S(1)} fusion(bf16[2048,2,2048]{2,0,1:T(8,128)(2,1)} %all-gather.17.cloned.1.call-done, bf16[1024,2048]{1,0:T(8,128)(2,1)} %all-gather.15.cloned.1.call-done), kind=kOutput, calls=%fused_computation.67 | convolution fusion | flops 17179869184 | bytes 37748736 | tf_op jit(solution)/shard_map/td,djf->tjf/dot_general | solution.py:181
  557.2 94.6 %all-gather.19.cloned.1.call-done = bf16[2048,2048]{1,0:T(8,128)(2,1)} async-done(((bf16[2048,256]{1,0:T(8,128)(2,1)}), bf16[2048,2048]{1,0:T(8,128)(2,1)}) %all-gather.19.cloned.1.call-update) | async-done | bytes 8388624 | tf_op jit(solution)/shard_map/all_gather | solution.py:162
  651.9 13.8 convolution_convert_fusion.3
  668.2 40.4 %reduce-scatter.11.cloned.1.call-done = bf16[256,2048]{1,0:T(8,128)(2,1)} async-done(((bf16[1024,2048]{1,0:T(8,128)(2,1)}), bf16[256,2048]{1,0:T(8,128)(2,1)}) %reduce-scatter.11.cloned.1.call-update) | async-done | bytes 1048592 | tf_op jit(solution)/shard_map/reduce_scatter | solution.py:186
  711.7 34.6 %all-gather.21.cloned.1.call-done = bf16[1024,2048]{1,0:T(8,128)(2,1)} async-done(((bf16[256,2048]{1,0:T(8,128)(2,1)}), bf16[1024,2048]{1,0:T(8,128)(2,1)}) %all-gather.21.cloned.1.call-update) | async-done | bytes 4194320 | tf_op jit(solution)/shard_map/all_gather | solution.py:200
  746.2 20.5 %fusion.46 = (bf16[1024,1,2048]{2,0,1:T(8,128)(2,1)}, bf16[1024,1,2048]{2,0,1:T(8,128)(2,1)}) fusion(f32[1024,2,2048]{2,0,1:T(8,128)} %copy-done.16, bf16[1024,2048]{1,0:T(8,128)(2,1)} %all-gather.21.cloned.1.call-done, bf16[2048,2048]{1,0:T(8,128)(2,1)} %all-gather.19.cloned.1.call-done), kind=kOutput, calls=%fused_computation.76 | convolution fusion | flops 8617197568 | bytes 37748736 | tf_op jit(solution)/shard_map/dot_general | solution.py:201
  766.7 23.9 %bitcast_convert_fusion.1 = bf16[1024,2048]{1,0:T(8,128)(2,1)} fusion(bf16[2048,2,2048]{2,0,1:T(8,128)(2,1)} %all-gather.17.cloned.1.call-done, bf16[1024,1,2048]{2,0,1:T(8,128)(2,1)} %get-tuple-element.287, bf16[1024,1,2048]{2,0,1:T(8,128)(2,1)} %get-tuple-element.286), kind=kOutput, calls=%fused_computation.54 | convolution fusion | flops 17186160640 | bytes 29360128 | tf_op jit(solution)/shard_map/tjf,djf->td/dot_general | solution.py:209
  790.7 44.7 %reduce-scatter.13.cloned.1.call-done = bf16[256,2048]{1,0:T(8,128)(2,1)} async-done(((bf16[1024,2048]{1,0:T(8,128)(2,1)}), bf16[256,2048]{1,0:T(8,128)(2,1)}) %reduce-scatter.13.cloned.1.call-update) | async-done | bytes 1048592 | tf_op jit(solution)/shard_map/reduce_scatter | solution.py:213
  842.8 14.5 convolution_convert_fusion.1
  863.2 14.2 all-gather.23.cloned.1.call-done
  889.7 52.0 %while.30 = (s32[]{:T(128)}, f32[1024,4,128]{0,2,1:T(8,128)S(1)}, f32[1024,4,128]{0,2,1:T(8,128)}, f32[2,512,4,128]{3,1,2,0:T(8,128)}, s32[2]{0:T(128)S(1)}, /*i...) while((s32[]{:T(128)}, f32[1024,4,128]{0,2,1:T(8,128)S(1)}, ...), condition=%wide.region_16.17_spmd.clone.clone, body=%wide.region_14.16_spmd.clone.sunk.clone | while | flops 2719743488 | bytes 180419536 | solution.py:109
  996.9 24.7 %convolution_convert_fusion = bf16[2048,2,2048]{2,0,1:T(8,128)(2,1)} fusion(bf16[1024,1,2048]{2,0,1:T(8,128)(2,1)} %get-tuple-element.287, bf16[1024,1,2048]{2,0,1:T(8,128)(2,1)} %get-tuple-element.286, bf16[1024,2048]{1,0:T(8,128)(2,1)} %all-gather.15.cloned.1.call-done), kind=kOutput, calls=%fused_computation.49 | convolution fusion | flops 17205035008 | bytes 29360128 | tf_op jit(solution)/shard_map/td,tjf->djf/dot_general | solution.py:212
  1021.7 40.7 %psum.7 = f32[]{:T(128)} all-reduce(f32[]{:T(128)} %get-tuple-element.226), channel_id=1, replica_groups=mesh['seq'=4,'fsdp'=8] {'seq','fsdp'}, use_global_device_ids=true, to_apply=%region_21.22 | all-reduce | flops 1 | bytes 8 | tf_op jit(solution)/shard_map/psum | solution.py:190
  1068.9 31.1 %reduce-scatter.19.cloned.1.call-done = bf16[512,256]{1,0:T(8,128)(2,1)} async-done(((bf16[512,2048]{1,0:T(8,128)(2,1)}), bf16[512,256]{1,0:T(8,128)(2,1)}) %reduce-scatter.19.cloned.1.call-update) | async-done | bytes 262160 | tf_op jit(solution)/shard_map/reduce_scatter | solution.py:248
  1102.6 43.9 %reduce-scatter.15.cloned.1.call-done = bf16[256,2048]{1,0:T(8,128)(2,1)} async-done(((bf16[1024,2048]{1,0:T(8,128)(2,1)}), bf16[256,2048]{1,0:T(8,128)(2,1)}) %reduce-scatter.15.cloned.1.call-update) | async-done | bytes 1048592 | tf_op jit(solution)/shard_map/reduce_scatter | solution.py:240
  1150.4 118.1 %reduce-scatter.17.cloned.1.call-done = bf16[256,3,512]{2,0,1:T(8,128)(2,1)} async-done(((bf16[2048,3,512]{2,0,1:T(8,128)(2,1)}), bf16[256,3,512]{2,0,1:T(8,128)(2,1)}) %reduce-scatter.17.cloned.1.call-update) | async-done | bytes 786448 | tf_op jit(solution)/shard_map/reduce_scatter | solution.py:245
  1273.9 276.9 %reduce-scatter.21.cloned.1.call-done = bf16[256,2,2048]{2,0,1:T(8,128)(2,1)} async-done(((bf16[2048,2,2048]{2,0,1:T(8,128)(2,1)}), bf16[256,2,2048]{2,0,1:T(8,128)(2,1)}) %reduce-scatter.21.cloned.1.call-update) | async-done | bytes 2097168 | tf_op jit(solution)/shard_map/reduce_scatter | solution.py:251
  1550.8 13.7 fusion.44
  (262 shorter events, 260.0 us)
Async XLA Ops:
  7.2 42.5 %all-gather.9.cloned.1.call-start = ((), (), s32[]{:S(2)}) async-start(), calls=%async_computation.8 | async-start | bytes 5242880 | tf_op jit(solution)/shard_map/all_gather | solution.py:165
  12.4 139.5 %all-gather.11.cloned.1.call-start = ((), (), s32[]{:S(2)}) async-start(), calls=%async_computation.9 | async-start | bytes 7077888 | tf_op jit(solution)/shard_map/all_gather | solution.py:159
  13.6 195.1 %all-gather.13.cloned.1.call-start = ((), (), s32[]{:S(2)}) async-start(), calls=%async_computation.10 | async-start | bytes 2359296 | tf_op jit(solution)/shard_map/all_gather | solution.py:160
  14.5 243.5 %reduce-scatter.9.cloned.1.call-start = ((), (), s32[]{:S(2)}) async-start(), calls=%async_computation.11 | async-start | bytes 5242880 | tf_op jit(solution)/shard_map/reduce_scatter | solution.py:176
  204.9 10.1 copy-start.3
  215.0 81.1 %all-gather.15.cloned.1.call-start = ((), (), s32[]{:S(2)}) async-start(), calls=%async_computation.12 | async-start | bytes 5242880 | tf_op jit(solution)/shard_map/all_gather | solution.py:180
  261.6 264.5 %all-gather.17.cloned.1.call-start = ((), (), s32[]{:S(2)}) async-start(), calls=%async_computation.13 | async-start | bytes 18874368 | tf_op jit(solution)/shard_map/all_gather | solution.py:161
  267.4 384.5 %all-gather.19.cloned.1.call-start = ((), (), s32[]{:S(2)}) async-start(), calls=%async_computation.14 | async-start | bytes 9437184 | tf_op jit(solution)/shard_map/all_gather | solution.py:162
  270.3 438.2 %reduce-scatter.11.cloned.1.call-start = ((), (), s32[]{:S(2)}) async-start(), calls=%async_computation.15 | async-start | bytes 5242880 | tf_op jit(solution)/shard_map/reduce_scatter | solution.py:186
  665.6 42.9 %copy-start.17 = (bf16[1,256,2048]{2,1,0:T(8,128)(2,1)S(1)}, bf16[1,256,2048]{2,1,0:T(8,128)(2,1)}, u32[]{:S(2)}) copy-start(bf16[1,256,2048]{2,1,0:T(8,128)(2,1)} %param.20) | copy-start | bytes 3145732
  665.7 80.6 %all-gather.21.cloned.1.call-start = ((), (), s32[]{:S(2)}) async-start(), calls=%async_computation.16 | async-start | bytes 5242880 | tf_op jit(solution)/shard_map/all_gather | solution.py:200
  711.6 123.8 %reduce-scatter.13.cloned.1.call-start = ((), (), s32[]{:S(2)}) async-start(), calls=%async_computation.17 | async-start | bytes 5242880 | tf_op jit(solution)/shard_map/reduce_scatter | solution.py:213
  790.6 86.7 %all-gather.23.cloned.1.call-start = ((), (), s32[]{:S(2)}) async-start(), calls=%async_computation.18 | async-start | bytes 5242880 | tf_op jit(solution)/shard_map/all_gather | solution.py:217
  842.7 220.3 %reduce-scatter.23.cloned.1.call-start = ((), (), s32[]{:S(2)}) async-start(), calls=%async_computation.23 | async-start | bytes 9437184 | tf_op jit(solution)/shard_map/reduce_scatter | solution.py:254
  857.3 242.6 %reduce-scatter.19.cloned.1.call-start = ((), (), s32[]{:S(2)}) async-start(), calls=%async_computation.21 | async-start | bytes 2359296 | tf_op jit(solution)/shard_map/reduce_scatter | solution.py:248
  860.0 17.3 %copy-start.34 = (bf16[2,512,4,128]{3,2,1,0:T(4,128)(2,1)S(1)}, bf16[2,512,4,128]{3,2,1,0:T(4,128)(2,1)}, u32[]{:S(2)}) copy-start(bf16[2,512,4,128]{3,2,1,0:T(4,128)(2,1)} %copy.65) | copy-start | bytes 3145732
  883.3 263.2 %reduce-scatter.15.cloned.1.call-start = ((), (), s32[]{:S(2)}) async-start(), calls=%async_computation.19 | async-start | bytes 5242880 | tf_op jit(solution)/shard_map/reduce_scatter | solution.py:240
  983.9 284.5 %reduce-scatter.17.cloned.1.call-start = ((), (), s32[]{:S(2)}) async-start(), calls=%async_computation.20 | async-start | bytes 7077888 | tf_op jit(solution)/shard_map/reduce_scatter | solution.py:245
  996.9 553.9 %reduce-scatter.21.cloned.1.call-start = ((), (), s32[]{:S(2)}) async-start(), calls=%async_computation.22 | async-start | bytes 18874368 | tf_op jit(solution)/shard_map/reduce_scatter | solution.py:251
  1021.7 41.4 %copy-start.21 = (f32[2048,256]{1,0:T(8,128)S(1)}, f32[2048,256]{1,0:T(8,128)}, u32[]{:S(2)}) copy-start(f32[2048,256]{1,0:T(8,128)} %param.25) | copy-start | bytes 6291460
  1068.9 77.7 %copy-start.6 = (bf16[1,256,2048]{2,1,0:T(8,128)(2,1)S(1)}, bf16[1,256,2048]{2,1,0:T(8,128)(2,1)}, u32[]{:S(2)}) copy-start(bf16[1,256,2048]{2,1,0:T(8,128)(2,1)} %param.19) | copy-start | bytes 3145732
  1068.9 77.7 %copy-start.42 = (f32[256]{0:T(256)S(1)}, f32[256]{0:T(256)}, u32[]{:S(2)}) copy-start(f32[256]{0:T(256)} %copy-done.41) | copy-start | bytes 3076
  1068.9 77.7 %copy-start.44 = (f32[256]{0:T(256)S(1)}, f32[256]{0:T(256)}, u32[]{:S(2)}) copy-start(f32[256]{0:T(256)} %copy-done.43) | copy-start | bytes 3076
  1068.9 79.7 %copy-start.22 = (f32[256,2048]{1,0:T(8,128)S(1)}, f32[256,2048]{1,0:T(8,128)}, u32[]{:S(2)}) copy-start(f32[256,2048]{1,0:T(8,128)} %get-tuple-element.281) | copy-start | bytes 6291460
  (50 other events, 194.9 us)
Sparse Core Ops, SparseCore 0:
  12.5 37.1 all-gather.8
  52.3 99.4 all-gather.10
  154.5 48.5 all-gather.12
  215.2 42.7 reduce-scatter.8
  261.7 34.4 all-gather.14
  298.8 227.2 all-gather.16
  528.7 123.1 all-gather.18
  665.8 42.7 reduce-scatter.10
  711.7 34.4 all-gather.20
  790.8 44.5 reduce-scatter.12
  842.8 34.4 all-gather.22
  880.8 147.8 reduce-scatter.22
  1032.2 67.6 reduce-scatter.18
  1102.9 43.5 reduce-scatter.14
  1150.0 118.4 reduce-scatter.16
  1272.1 278.7 reduce-scatter.20
where the time goes:
time: 1590 us
  waiting for transfers between devices  1130 us (71%)
  matrix products  215 us (14%)
  other arithmetic  98.9 us (6%)
  local copies, waits for them, and re-layouts  78.1 us (5%)
  blocking collectives  40.7 us (3%)
  between operations  17.1 us (1%)
    reduce_scatter x1, waiting for transfers between devices, on_device(): lax.psum_scatter(grad_gateup.astype(jnp.bfloat16), 'fsdp', scatter_dimens...  277 us
    all_gather x1, waiting for transfers between devices, on_device(): lax.all_gather(low_weights[2], 'fsdp', axis=0, tiled=True)  230 us
    reduce_scatter x1, waiting for transfers between devices, on_device(): lax.psum_scatter(grad_qkv.astype(jnp.bfloat16), 'fsdp', scatter_dimension...  118 us
    all_gather x1, waiting for transfers between devices, on_device(): lax.all_gather(low_weights[0], 'fsdp', axis=0, tiled=True)  102 us
    all_gather x1, waiting for transfers between devices, on_device(): lax.all_gather(low_weights[3], 'fsdp', axis=1, tiled=True)  94.6 us
    reduce_scatter x1, waiting for transfers between devices, on_device(): lax.psum_scatter(normed_grad_two.astype(jnp.bfloat16), 'seq', scatter_dim...  44.7 us
    reduce_scatter x1, waiting for transfers between devices, on_device(): lax.psum_scatter(normed_grad_one.astype(jnp.bfloat16), 'seq', scatter_dim...  43.9 us
    reduce_scatter x1, waiting for transfers between devices, on_device(): lax.psum_scatter(attn_term.astype(jnp.bfloat16), 'seq', scatter_dimension...  42.9 us
  transfers between devices with their start and end apart: 16, of which 14 were waited for; matrix products, arithmetic and copies ran while one was open for 17% of the time, Pallas kernels for 0%

commit v1 on v0

--- a/solution.py
+++ b/solution.py
@@ -9,6 +9,26 @@
 MOMENT = 0.9
 KEEP = 0.95
 NEG = -1e30
+
+
+def recover_slots(panel, at_axis):
+    base_arr = list(panel.shape[1:])
+    base_arr[at_axis] *= panel.shape[0]
+    front = jnp.moveaxis(panel, 0, at_axis).reshape(base_arr)
+    return front
+
+
+def tiles_end(xin, ax_name):
+    n_parts = jax.lax.axis_size(ax_name)
+    frame_out = xin[None]
+    for m in range(n_parts.bit_length() - 1):
+        s_next = 1 << m
+        small = tuple(((k0, k0 ^ s_next) for k0 in range(n_parts)))
+        fresh = jax.lax.ppermute(frame_out, axis_name=ax_name, perm=small)
+        now = jnp.stack([frame_out, fresh])
+        then = jax.lax.axis_index(ax_name) >> m & 1
+        frame_out = jnp.where(then == 0, now, now[::-1]).reshape(-1, *xin.shape)
+    return frame_out
 
 
 def layer_norm(values):
@@ -155,11 +175,17 @@
         w_gateup.astype(jnp.bfloat16),
         w_down.astype(jnp.bfloat16),
     )
+
+    def views_handle(payload, sample, ndim_at):
+        u1 = tiles_end(payload, sample)
+        piece_out = recover_slots(u1, ndim_at)
+        return piece_out
+
     full_qkv, full_out, full_gateup, full_down = (
         lax.all_gather(low_weights[0], "fsdp", axis=0, tiled=True),
         lax.all_gather(low_weights[1], "fsdp", axis=1, tiled=True),
         lax.all_gather(low_weights[2], "fsdp", axis=0, tiled=True),
-        lax.all_gather(low_weights[3], "fsdp", axis=1, tiled=True),
+        views_handle(low_weights[3], "fsdp", 1),
     )
     normed_one, factor_one = layer_norm(inputs)
     group_one = lax.all_gather(normed_one.astype(jnp.bfloat16), "seq", axis=0, tiled=True)

time: 1590 us -> 1850 us (1.16)
  waiting for transfers between devices: 1130 us -> 1340 us
  other arithmetic: 98.9 us -> 130 us
    ppermute x0 -> x3, waiting for transfers between devices: none -> 437 us  [tiles_end(): fresh = jax.lax.ppermute(frame_out, axis_name=ax_name, perm=small)]
    all_gather x1, waiting for transfers between devices: 230 us -> 0.01 us  [on_device(): lax.all_gather(low_weights[2], 'fsdp', axis=0, tiled=True)]
    all_gather x1, waiting for transfers between devices: 94.6 us -> 125 us  [on_device(): lax.all_gather(low_weights[3], 'fsdp', axis=1, tiled=True)]
    all_gather x1, waiting for transfers between devices: 25.8 us -> 0.01 us  [on_device(): lax.all_gather(normed_two.astype(jnp.bfloat16), 'seq', axis=0, tiled=True)]
  transfers between devices with their start and end apart: 16 -> 19, of which waited for: 14 -> 15; matrix products, arithmetic and copies ran while one was open for 17% -> 16% of each run, Pallas kernels for 0% -> 0%
where the time goes in v1:
time: 1850 us
  waiting for transfers between devices  1340 us (72%)
  matrix products  222 us (12%)
  other arithmetic  130 us (7%)
  local copies, waits for them, and re-layouts  85.5 us (5%)
  blocking collectives  40.8 us (2%)
    ppermute x3, waiting for transfers between devices, tiles_end(): fresh = jax.lax.ppermute(frame_out, axis_name=ax_name, perm=small)  437 us
    reduce_scatter x1, waiting for transfers between devices, on_device(): lax.psum_scatter(grad_gateup.astype(jnp.bfloat16), 'fsdp', scatter_dimens...  277 us
    all_gather x1, waiting for transfers between devices, on_device(): lax.all_gather(low_weights[3], 'fsdp', axis=1, tiled=True)  125 us
    reduce_scatter x1, waiting for transfers between devices, on_device(): lax.psum_scatter(grad_qkv.astype(jnp.bfloat16), 'fsdp', scatter_dimension...  118 us
    all_gather x1, waiting for transfers between devices, on_device(): lax.all_gather(low_weights[0], 'fsdp', axis=0, tiled=True)  102 us
    reduce_scatter x1, waiting for transfers between devices, on_device(): lax.psum_scatter(normed_grad_two.astype(jnp.bfloat16), 'seq', scatter_dim...  44.7 us
    reduce_scatter x1, waiting for transfers between devices, on_device(): lax.psum_scatter(normed_grad_one.astype(jnp.bfloat16), 'seq', scatter_dim...  43.9 us
    reduce_scatter x1, waiting for transfers between devices, on_device(): lax.psum_scatter(attn_term.astype(jnp.bfloat16), 'seq', scatter_dimension...  42.9 us
  transfers between devices with their start and end apart: 19, of which 15 were waited for; matrix products, arithmetic and copies ran while one was open for 16% of the time, Pallas kernels for 0%

profile of v1, /device:TPU:0, one launch (start us, length us, event | category | flops | bytes accessed | tf_op | source)
XLA Modules:
  0.0 1847.6 jit_solution(13149718555216796241)
XLA Ops:
  19.5 30.2 %all-gather.9.cloned.1.call-done = bf16[1024,2048]{1,0:T(8,128)(2,1)} async-done(((bf16[256,2048]{1,0:T(8,128)(2,1)}), bf16[1024,2048]{1,0:T(8,128)(2,1)}) %all-gather.9.cloned.1.call-update) | async-done | bytes 4194320 | tf_op jit(solution)/shard_map/all_gather | solution.py:191
  49.8 102.1 %all-gather.11.cloned.1.call-done = bf16[2048,3,512]{0,2,1:T(8,128)(2,1)} async-done(((bf16[256,3,512]{0,2,1:T(8,128)(2,1)}), bf16[2048,3,512]{0,2,1:T(8,128)(2,1)}) %all-gather.11.cloned.1.call-update) | async-done | bytes 6291472 | tf_op jit(solution)/shard_map/all_gather | solution.py:185
  180.5 24.6 %while.29 = (s32[]{:T(128)}, bf16[2,512,4,128]{3,1,2,0:T(8,128)(2,1)}, f32[2,4,512]{2,1,0:T(4,128)S(1)}, s32[2]{0:T(128)S(1)}, s32[]{:T(128)}, /*index=5*/bf16[1...) while((s32[]{:T(128)}, ...), condition=%wide.region_5.6_spmd.clone, body=%wide.region_2.5_spmd.sunk.clone | while | flops 1099955712 | bytes 35199660 | solution.py:89
  215.2 42.9 %reduce-scatter.9.cloned.1.call-done = bf16[256,2048]{1,0:T(8,128)(2,1)} async-done(((bf16[1024,2048]{1,0:T(8,128)(2,1)}), bf16[256,2048]{1,0:T(8,128)(2,1)}) %reduce-scatter.9.cloned.1.call-update) | async-done | bytes 1048592 | tf_op jit(solution)/shard_map/reduce_scatter | solution.py:202
  273.4 21.6 %collective-permute-done = bf16[1,2048,256]{2,1,0:T(8,128)(2,1)} collective-permute-done((bf16[1,2048,256]{2,1,0:T(8,128)(2,1)S(1)}, bf16[1,2048,256]{2,1,0:T(8,128)(2,1)}, u32[]{:S(2)}, u32[]{:S(2)}) %collective-permute-start) | collective-permute-done | bytes 1048608 | tf_op jit(solution)/shard_map/ppermute | solution.py:27
  300.3 112.6 %collective-permute-done.1 = bf16[2,2048,256]{2,1,0:T(8,128)(2,1)} collective-permute-done((bf16[2,2048,256]{2,1,0:T(8,128)(2,1)}, bf16[2,2048,256]{2,1,0:T(8,128)(2,1)}, u32[]{:S(2)}, u32[]{:S(2)}) %collective-permute-start.1) | collective-permute-done | bytes 2097184 | tf_op jit(solution)/shard_map/ppermute | solution.py:27
  432.9 302.4 %collective-permute-done.2 = bf16[4,2048,256]{1,2,0:T(8,128)(2,1)} collective-permute-done((bf16[4,2048,256]{1,2,0:T(8,128)(2,1)}, bf16[4,2048,256]{1,2,0:T(8,128)(2,1)}, u32[]{:S(2)}, u32[]{:S(2)}) %collective-permute-start.2) | collective-permute-done | bytes 4194336 | tf_op jit(solution)/shard_map/ppermute | solution.py:27
  742.9 14.4 reverse_select_fusion
  757.3 23.5 %fusion.52 = f32[1024,2,2048]{2,0,1:T(8,128)} fusion(bf16[2048,2,2048]{2,0,1:T(8,128)(2,1)} %all-gather.17.cloned.1.call-done, bf16[1024,2048]{1,0:T(8,128)(2,1)} %all-gather.15.cloned.1.call-done), kind=kOutput, calls=%fused_computation.84 | convolution fusion | flops 17179869184 | bytes 37748736 | tf_op jit(solution)/shard_map/td,djf->tjf/dot_general | solution.py:207
  780.8 17.4 fusion.61
  803.1 38.9 %reduce-scatter.11.cloned.1.call-done = bf16[256,2048]{1,0:T(8,128)(2,1)} async-done(((bf16[1024,2048]{1,0:T(8,128)(2,1)}), bf16[256,2048]{1,0:T(8,128)(2,1)}) %reduce-scatter.11.cloned.1.call-update) | async-done | bytes 1048592 | tf_op jit(solution)/shard_map/reduce_scatter | solution.py:212
  845.1 124.5 %all-gather.21.cloned.1.call-done = bf16[2048,2048]{1,0:T(8,128)(2,1)} async-done(((bf16[2048,256]{1,0:T(8,128)(2,1)}), bf16[2048,2048]{1,0:T(8,128)(2,1)}) %all-gather.21.cloned.1.call-update) | async-done | bytes 8388624 | tf_op jit(solution)/shard_map/all_gather | solution.py:222
  969.6 34.8 %all-gather.19.cloned.1.call-done = bf16[1024,2048]{1,0:T(8,128)(2,1)} async-done(((bf16[256,2048]{1,0:T(8,128)(2,1)}), bf16[1024,2048]{1,0:T(8,128)(2,1)}) %all-gather.19.cloned.1.call-update) | async-done | bytes 4194320 | tf_op jit(solution)/shard_map/all_gather | solution.py:226
  1004.4 20.7 %fusion.60 = (bf16[1024,1,2048]{2,0,1:T(8,128)(2,1)}, bf16[1024,1,2048]{2,0,1:T(8,128)(2,1)}) fusion(f32[1024,2,2048]{2,0,1:T(8,128)} %fusion.52, bf16[1024,2048]{1,0:T(8,128)(2,1)} %all-gather.19.cloned.1.call-done, bf16[2048,2048]{1,0:T(8,128)(2,1)} %all-gather.21.cloned.1.call-done), kind=kOutput, calls=%fused_computation.93 | convolution fusion | flops 8617197568 | bytes 37748736 | tf_op jit(solution)/shard_map/dot_general | solution.py:227
  1025.1 23.8 %bitcast_convert_fusion.1 = bf16[1024,2048]{1,0:T(8,128)(2,1)} fusion(bf16[2048,2,2048]{2,0,1:T(8,128)(2,1)} %all-gather.17.cloned.1.call-done, bf16[1024,1,2048]{2,0,1:T(8,128)(2,1)} %get-tuple-element.287, bf16[1024,1,2048]{2,0,1:T(8,128)(2,1)} %get-tuple-element.286), kind=kOutput, calls=%fused_computation.54 | convolution fusion | flops 17186160640 | bytes 29360128 | tf_op jit(solution)/shard_map/tjf,djf->td/dot_general | solution.py:235
  1048.9 44.7 %reduce-scatter.13.cloned.1.call-done = bf16[256,2048]{1,0:T(8,128)(2,1)} async-done(((bf16[1024,2048]{1,0:T(8,128)(2,1)}), bf16[256,2048]{1,0:T(8,128)(2,1)}) %reduce-scatter.13.cloned.1.call-update) | async-done | bytes 1048592 | tf_op jit(solution)/shard_map/reduce_scatter | solution.py:239
  1101.1 16.2 convolution_convert_fusion.1
  1147.9 52.1 %while.30 = (s32[]{:T(128)}, f32[1024,4,128]{0,2,1:T(8,128)S(1)}, f32[1024,4,128]{0,2,1:T(8,128)}, f32[2,512,4,128]{3,1,2,0:T(8,128)}, s32[2]{0:T(128)S(1)}, /*i...) while((s32[]{:T(128)}, f32[1024,4,128]{0,2,1:T(8,128)S(1)}, ...), condition=%wide.region_16.17_spmd.clone.clone, body=%wide.region_14.16_spmd.clone.sunk.clone | while | flops 2719743488 | bytes 180419536 | solution.py:129
  1255.2 24.7 %convolution_convert_fusion = bf16[2048,2,2048]{2,0,1:T(8,128)(2,1)} fusion(bf16[1024,1,2048]{2,0,1:T(8,128)(2,1)} %get-tuple-element.287, bf16[1024,1,2048]{2,0,1:T(8,128)(2,1)} %get-tuple-element.286, bf16[1024,2048]{1,0:T(8,128)(2,1)} %all-gather.15.cloned.1.call-done), kind=kOutput, calls=%fused_computation.50 | convolution fusion | flops 17205035008 | bytes 29360128 | tf_op jit(solution)/shard_map/td,tjf->djf/dot_general | solution.py:238
  1279.9 40.8 %psum.7 = f32[]{:T(128)} all-reduce(f32[]{:T(128)} %get-tuple-element.226), channel_id=1, replica_groups=mesh['seq'=4,'fsdp'=8] {'seq','fsdp'}, use_global_device_ids=true, to_apply=%region_21.22 | all-reduce | flops 1 | bytes 8 | tf_op jit(solution)/shard_map/psum | solution.py:216
  1327.2 31.8 %reduce-scatter.19.cloned.1.call-done = bf16[512,256]{1,0:T(8,128)(2,1)} async-done(((bf16[512,2048]{1,0:T(8,128)(2,1)}), bf16[512,256]{1,0:T(8,128)(2,1)}) %reduce-scatter.19.cloned.1.call-update) | async-done | bytes 262160 | tf_op jit(solution)/shard_map/reduce_scatter | solution.py:274
  1361.7 43.9 %reduce-scatter.15.cloned.1.call-done = bf16[256,2048]{1,0:T(8,128)(2,1)} async-done(((bf16[1024,2048]{1,0:T(8,128)(2,1)}), bf16[256,2048]{1,0:T(8,128)(2,1)}) %reduce-scatter.15.cloned.1.call-update) | async-done | bytes 1048592 | tf_op jit(solution)/shard_map/reduce_scatter | solution.py:266
  1409.4 118.1 %reduce-scatter.17.cloned.1.call-done = bf16[256,3,512]{2,0,1:T(8,128)(2,1)} async-done(((bf16[2048,3,512]{2,0,1:T(8,128)(2,1)}), bf16[256,3,512]{2,0,1:T(8,128)(2,1)}) %reduce-scatter.17.cloned.1.call-update) | async-done | bytes 786448 | tf_op jit(solution)/shard_map/reduce_scatter | solution.py:271
  1533.0 277.0 %reduce-scatter.21.cloned.1.call-done = bf16[256,2,2048]{2,0,1:T(8,128)(2,1)} async-done(((bf16[2048,2,2048]{2,0,1:T(8,128)(2,1)}), bf16[256,2,2048]{2,0,1:T(8,128)(2,1)}) %reduce-scatter.21.cloned.1.call-update) | async-done | bytes 2097168 | tf_op jit(solution)/shard_map/reduce_scatter | solution.py:277
  (283 shorter events, 314.7 us)
Async XLA Ops:
  7.2 42.6 %all-gather.9.cloned.1.call-start = ((), (), s32[]{:S(2)}) async-start(), calls=%async_computation.8 | async-start | bytes 5242880 | tf_op jit(solution)/shard_map/all_gather | solution.py:191
  12.4 139.5 %all-gather.11.cloned.1.call-start = ((), (), s32[]{:S(2)}) async-start(), calls=%async_computation.9 | async-start | bytes 7077888 | tf_op jit(solution)/shard_map/all_gather | solution.py:185
  13.7 195.2 %all-gather.13.cloned.1.call-start = ((), (), s32[]{:S(2)}) async-start(), calls=%async_computation.10 | async-start | bytes 2359296 | tf_op jit(solution)/shard_map/all_gather | solution.py:186
  14.5 243.6 %reduce-scatter.9.cloned.1.call-start = ((), (), s32[]{:S(2)}) async-start(), calls=%async_computation.11 | async-start | bytes 5242880 | tf_op jit(solution)/shard_map/reduce_scatter | solution.py:202
  215.2 542.2 %all-gather.15.cloned.1.call-start = ((), (), s32[]{:S(2)}) async-start(), calls=%async_computation.12 | async-start | bytes 5242880 | tf_op jit(solution)/shard_map/all_gather | solution.py:206
  262.3 495.0 %all-gather.17.cloned.1.call-start = ((), (), s32[]{:S(2)}) async-start(), calls=%async_computation.13 | async-start | bytes 18874368 | tf_op jit(solution)/shard_map/all_gather | solution.py:187
  268.1 573.9 %reduce-scatter.11.cloned.1.call-start = ((), (), s32[]{:S(2)}) async-start(), calls=%async_computation.14 | async-start | bytes 5242880 | tf_op jit(solution)/shard_map/reduce_scatter | solution.py:212
  270.0 24.9 %collective-permute-start = (bf16[1,2048,256]{2,1,0:T(8,128)(2,1)S(1)}, bf16[1,2048,256]{2,1,0:T(8,128)(2,1)}, u32[]{:S(2)}, u32[]{:S(2)}) collective-permute-start(bf16[1,2048,256]{2,1,0:T(8,128)(2,1)S(1)} %convert_bitcast_fusion.2), channel_id=1, source_target_pairs={{0,1},{1,0},{2,3},{3,2},{4,5},{5,4},{6,7},{7,6},{8,9},{9,8},{10,11... | collective-permute-start | bytes 3145736 | tf_op jit(solution)/shard_map/ppermute | solution.py:27
  298.8 114.1 %collective-permute-start.1 = (bf16[2,2048,256]{2,1,0:T(8,128)(2,1)}, bf16[2,2048,256]{2,1,0:T(8,128)(2,1)}, u32[]{:S(2)}, u32[]{:S(2)}) collective-permute-start(bf16[2,2048,256]{2,1,0:T(8,128)(2,1)} %get-tuple-element.301), channel_id=1, source_target_pairs={{0,2},{1,3},{2,0},{3,1},{4,6},{5,7},{6,4},{7,5},{8,10},{9,11},{10,... | collective-permute-start | bytes 6291464 | tf_op jit(solution)/shard_map/ppermute | solution.py:27
  425.6 309.7 %collective-permute-start.2 = (bf16[4,2048,256]{1,2,0:T(8,128)(2,1)}, bf16[4,2048,256]{1,2,0:T(8,128)(2,1)}, u32[]{:S(2)}, u32[]{:S(2)}) collective-permute-start(bf16[4,2048,256]{1,2,0:T(8,128)(2,1)} %copy.67), channel_id=1, source_target_pairs={{0,4},{1,5},{2,6},{3,7},{4,0},{5,1},{6,2},{7,3},{8,12},{9,13},{10,... | collective-permute-start | bytes 12582920 | tf_op jit(solution)/shard_map/ppermute | solution.py:27
  798.3 171.3 %all-gather.21.cloned.1.call-start = ((), (), s32[]{:S(2)}) async-start(), calls=%async_computation.16 | async-start | bytes 9437184 | tf_op jit(solution)/shard_map/all_gather | solution.py:222
  801.1 203.3 %all-gather.19.cloned.1.call-start = ((), (), s32[]{:S(2)}) async-start(), calls=%async_computation.15 | async-start | bytes 5242880 | tf_op jit(solution)/shard_map/all_gather | solution.py:226
  845.0 248.6 %reduce-scatter.13.cloned.1.call-start = ((), (), s32[]{:S(2)}) async-start(), calls=%async_computation.17 | async-start | bytes 5242880 | tf_op jit(solution)/shard_map/reduce_scatter | solution.py:239
  1048.9 44.8 %copy-start.47 = (f32[256]{0:T(256)S(1)}, f32[256]{0:T(256)}, u32[]{:S(2)}) copy-start(f32[256]{0:T(256)} %copy-done.46) | copy-start | bytes 3076
  1048.9 86.8 %all-gather.23.cloned.1.call-start = ((), (), s32[]{:S(2)}) async-start(), calls=%async_computation.18 | async-start | bytes 5242880 | tf_op jit(solution)/shard_map/all_gather | solution.py:243
  1101.0 220.3 %reduce-scatter.23.cloned.1.call-start = ((), (), s32[]{:S(2)}) async-start(), calls=%async_computation.23 | async-start | bytes 9437184 | tf_op jit(solution)/shard_map/reduce_scatter | solution.py:280
  1117.4 241.7 %reduce-scatter.19.cloned.1.call-start = ((), (), s32[]{:S(2)}) async-start(), calls=%async_computation.21 | async-start | bytes 2359296 | tf_op jit(solution)/shard_map/reduce_scatter | solution.py:274
  1141.6 264.0 %reduce-scatter.15.cloned.1.call-start = ((), (), s32[]{:S(2)}) async-start(), calls=%async_computation.19 | async-start | bytes 5242880 | tf_op jit(solution)/shard_map/reduce_scatter | solution.py:266
  1242.4 285.1 %reduce-scatter.17.cloned.1.call-start = ((), (), s32[]{:S(2)}) async-start(), calls=%async_computation.20 | async-start | bytes 7077888 | tf_op jit(solution)/shard_map/reduce_scatter | solution.py:271
  1255.1 554.8 %reduce-scatter.21.cloned.1.call-start = ((), (), s32[]{:S(2)}) async-start(), calls=%async_computation.22 | async-start | bytes 18874368 | tf_op jit(solution)/shard_map/reduce_scatter | solution.py:277
  1327.2 78.4 %copy-start.6 = (bf16[1,256,2048]{2,1,0:T(8,128)(2,1)S(1)}, bf16[1,256,2048]{2,1,0:T(8,128)(2,1)}, u32[]{:S(2)}) copy-start(bf16[1,256,2048]{2,1,0:T(8,128)(2,1)} %param.19) | copy-start | bytes 3145732
  1327.2 78.4 %copy-start.41 = (f32[256]{0:T(256)S(1)}, f32[256]{0:T(256)}, u32[]{:S(2)}) copy-start(f32[256]{0:T(256)} %copy-done.40) | copy-start | bytes 3076
  1327.2 78.4 %copy-start.45 = (f32[256]{0:T(256)S(1)}, f32[256]{0:T(256)}, u32[]{:S(2)}) copy-start(f32[256]{0:T(256)} %copy-done.44) | copy-start | bytes 3076
  1327.2 80.5 %copy-start.21 = (f32[256,2048]{1,0:T(8,128)S(1)}, f32[256,2048]{1,0:T(8,128)}, u32[]{:S(2)}) copy-start(f32[256,2048]{1,0:T(8,128)} %get-tuple-element.281) | copy-start | bytes 6291460
  (56 other events, 348.5 us)
Sparse Core Ops, SparseCore 0:
  12.5 37.1 all-gather.8
  52.4 99.4 all-gather.10
  154.5 48.5 all-gather.12
  215.3 42.7 reduce-scatter.8
  262.4 34.4 all-gather.14
  299.5 412.3 all-gather.16
  798.4 43.5 reduce-scatter.10
  844.6 124.9 all-gather.20
  971.7 32.6 all-gather.18
  1049.0 44.5 reduce-scatter.12
  1101.1 34.4 all-gather.22
  1139.1 147.8 reduce-scatter.22
  1290.6 68.4 reduce-scatter.18
  1362.0 43.5 reduce-scatter.14
  1409.1 118.4 reduce-scatter.16
  1531.2 278.7 reduce-scatter.20
